TPU v7x, 32 devices: a whole 2x2x4 slice. The times are simulated.
32 devices in a mesh: inner: 4 (over x, core), outer: 8 (over z, y).
Axes of the slice: x: 2, y: 2, z: 4, core: 2. Of those that a mesh axis runs over, the one named last changes fastest.
Arguments:
- tokens: bfloat16 [4096, 4096], P(('inner', 'outer')), may hold values from -6 to 6
- weight_codes: bfloat16 [4096, 512], P('inner'), may hold values from -127 to 127
- scales: float32 [1024], P('inner'), may hold values from 0.00012 to 0.0004
- cotangent: bfloat16 [4096, 512], P(('inner', 'outer')), may hold values from -6 to 6
Outputs:
- keys: bfloat16 [4096, 512], P(('inner', 'outer'))
- grad_tokens: bfloat16 [4096, 4096], P(('inner', 'outer'))
- grad_weight: float32 [4096, 512], P(('inner', 'outer'))
All inputs are finite; a program needn't handle non-finite values.
Results may differ from a plain program's by a relative error of at most 0.017.
Values may be sent and summed in bfloat16 or wider, within the bound.
No kernel may reach another device: no remote copies, remote signals or barrier semaphores. Data moves between devices by JAX's collectives and lax.ppermute only.
A program may use at most 64 MiB of HBM per device.

v0:
```python
import jax
import jax.numpy as jnp
from jax import lax
from jax.sharding import PartitionSpec as P

EPS = 1e-05


def local(tokens, weight_codes, scales, cotangent):
    kv_width = cotangent.shape[1]
    tok_rows = tokens.shape[0]
    block_rows = weight_codes.shape[0] // scales.shape[0]
    xf = tokens.astype(jnp.float32)
    inv_norm = lax.rsqrt(jnp.mean(xf * xf, axis=-1, keepdims=True) + EPS)
    normed_f = xf * inv_norm
    normed = normed_f.astype(jnp.bfloat16)
    packed = weight_codes.reshape(scales.shape[0], block_rows * kv_width)
    all_scales = lax.all_gather(scales, "inner", axis=0, tiled=True)
    code_piece = lax.all_gather(packed, "inner", axis=0, tiled=True)
    count_rows = code_piece.shape[0] * block_rows
    dequant = (code_piece.astype(jnp.float32) * all_scales[:, None]).reshape(count_rows, kv_width)
    dequant = dequant.astype(jnp.bfloat16)
    key_total = jnp.dot(normed, dequant, preferred_element_type=jnp.float32)
    grad_piece = lax.dot_general(
        cotangent, dequant, (((1,), (1,)), ((), ())), preferred_element_type=jnp.float32
    )
    grad_normed = grad_piece
    key_total, grad_normed = (key_total, grad_normed)
    received = lax.all_to_all(normed, "inner", split_axis=1, concat_axis=0, tiled=True)
    own_rows = received.shape[1]
    piece = lax.all_gather(cotangent, "inner", axis=0, tiled=True)
    blocks = piece.shape[0] // tok_rows
    slab = received
    slab = slab.reshape(blocks, tok_rows, own_rows)
    grads = piece.reshape(blocks, tok_rows, kv_width)
    parts = jnp.einsum("btr,btk->brk", slab, grads, preferred_element_type=jnp.float32)
    parts = lax.optimization_barrier(parts.astype(jnp.bfloat16)).astype(jnp.float32)
    group_sum = jnp.sum(parts, axis=0)
    grad_weight = lax.psum_scatter(group_sum, "outer", scatter_dimension=0, tiled=True)
    keys = key_total.astype(jnp.bfloat16)
    inner_mean = jnp.mean(grad_normed * normed_f, axis=-1, keepdims=True)
    grad_tokens = (inv_norm * (grad_normed - normed_f * inner_mean)).astype(jnp.bfloat16)
    return (keys, grad_tokens, grad_weight)


def solution(mesh):
    in_specs = (
        P(("inner", "outer"), None),
        P("inner", None),
        P("inner"),
        P(("inner", "outer"), None),
    )
    out_specs = (
        P(("inner", "outer"), None),
        P(("inner", "outer"), None),
        P(("inner", "outer"), None),
    )
    return jax.shard_map(local, mesh=mesh, in_specs=in_specs, out_specs=out_specs, check_vma=False)
```

profile of v0, /device:TPU:0, one launch (start us, length us, event | category | flops | bytes accessed | tf_op | source)
XLA Modules:
  0.0 165.0 jit_solution(4015287127052884973)
XLA Ops:
  7.2 0.0 copy-start.1
  7.2 0.0 all-gather.3.cloned.1.call-start
  7.2 2.5 %reshape.32 = bf16[256,2048]{1,0:T(8,128)(2,1)} reshape(bf16[1024,512]{1,0:T(8,128)(2,1)} %param.5) | data formatting | bytes 2097152 | tf_op jit(solution)/shard_map/reshape | solution.py:17
  9.7 0.0 all-gather.3.cloned.1.call-update
  9.7 1.6 copy.9
  11.4 0.0 copy-done.1
  11.4 6.0 %all-gather = f32[4,1,256]{2,1,0:T(1,128)S(1)} all-gather(f32[1,1,256]{2,1,0:T(1,128)S(1)} %bitcast.16), channel_id=1, replica_groups=mesh['inner'=4,'outer'=8] {'inner'}, dimensions={0}, use_global_device_ids=true | all-gather | bytes 5120 | tf_op jit(solution)/shard_map/all_gather | solution.py:18
  17.4 0.6 fusion.7
  17.9 29.4 %all-gather.3.cloned.1.call-done = bf16[1024,2048]{1,0:T(8,128)(2,1)} async-done(((bf16[256,2048]{1,0:T(8,128)(2,1)}), bf16[1024,2048]{1,0:T(8,128)(2,1)}) %all-gather.3.cloned.1.call-update) | async-done | bytes 4194320 | tf_op jit(solution)/shard_map/all_gather | solution.py:19
  47.3 4.9 %multiply_convert_fusion = bf16[1024,2048]{1,0:T(8,128)(2,1)} fusion(bf16[1024,2048]{1,0:T(8,128)(2,1)} %all-gather.3.cloned.1.call-done, f32[1024]{0:T(1024)S(1)} %bitcast.15), kind=kLoop, calls=%fused_computation.1 | loop fusion | flops 6291456 | bytes 8392704 | tf_op jit(solution)/shard_map/convert_element_type | solution.py:22
  52.2 0.0 copy-start
  52.2 7.6 %convert_element_type.31 = bf16[4096,512]{1,0:T(8,128)(2,1)} reshape(bf16[1024,2048]{1,0:T(8,128)(2,1)} %multiply_convert_fusion) | data formatting | bytes 8388608 | tf_op jit(solution)/shard_map/convert_element_type | solution.py:22
  59.8 0.0 copy-done
  59.8 3.5 %fusion.3 = (f32[128]{0:T(128)S(1)}, f32[128,4096]{0,1:T(8,128)S(1)}) fusion(bf16[128,4096]{0,1:T(8,128)(2,1)S(1)} %copy.9, f32[128]{0:T(128)S(1)} %add_rsqrt_fusion, bf16[4096,512]{1,0:T(8,128)(2,1)} %convert_element_type.31, bf16[128,512]{1,0:T(8,128)(2,1)S(1)} %copy-done), kind=kOutput, calls=%fused_computation.9 | convolution fusion | flops 538967936 | bytes 7472128 | tf_op jit(solution)/shard_map/dot_general | solution.py:24
  63.3 1.5 fusion.6
  64.8 3.5 %all-to-all-start = ((bf16[128,4,1024]{0,2,1:T(8,128)(2,1)}), bf16[128,4,1024]{0,2,1:T(8,128)(2,1)S(1)}, u32[]{:S(2)}, u32[]{:S(2)}) async-start(bf16[128,4,1024]{0,2,1:T(8,128)(2,1)} %bitcast.3), calls=%async_computation | async-start | bytes 2097152 | tf_op jit(solution)/shard_map/all_to_all | solution.py:29
  68.3 0.0 reduce-scatter.2.cloned.1.call-start
  68.3 18.0 %all_gather.11 = bf16[512,512]{1,0:T(8,128)(2,1)S(1)} all-gather(bf16[128,512]{1,0:T(8,128)(2,1)S(1)} %copy-done), channel_id=1, replica_groups=mesh['inner'=4,'outer'=8] {'inner'}, dimensions={0}, use_global_device_ids=true | all-gather | bytes 655360 | tf_op jit(solution)/shard_map/all_gather | solution.py:31
  86.4 0.0 all-to-all-done
  86.4 1.2 convolution_convert_fusion
  87.6 2.0 %convert_reduce_fusion = f32[1024,512]{1,0:T(8,128)} fusion(bf16[4,1024,512]{2,1,0:T(8,128)(2,1)S(1)} %convolution_convert_fusion), kind=kLoop, calls=%fused_computation | loop fusion | flops 3670016 | bytes 6291456 | tf_op jit(solution)/shard_map/reduce_sum | solution.py:38
  89.6 0.0 reduce-scatter.2.cloned.1.call-update
  89.6 1.3 copy.10
  90.9 3.9 %convolution_convert_fusion.1 = bf16[128,512]{1,0:T(8,128)(2,1)} fusion(bf16[128,4096]{0,1:T(8,128)(2,1)} %get-tuple-element.10, bf16[4096,512]{1,0:T(8,128)(2,1)} %convert_element_type.31), kind=kOutput, calls=%fused_computation.14 | convolution fusion | flops 536936448 | bytes 5373952 | tf_op jit(solution)/shard_map/dot_general | solution.py:23
  94.8 63.3 %reduce-scatter.2.cloned.1.call-done = f32[128,512]{1,0:T(8,128)} async-done(((f32[1024,512]{1,0:T(8,128)}), f32[128,512]{1,0:T(8,128)}) %reduce-scatter.2.cloned.1.call-update) | async-done | bytes 262160 | tf_op jit(solution)/shard_map/reduce_scatter | solution.py:39
  (2 shorter events, 0.0 us)
Async XLA Ops:
  7.2 4.2 %copy-start.1 = (f32[256]{0:T(256)S(1)}, f32[256]{0:T(256)}, u32[]{:S(2)}) copy-start(f32[256]{0:T(256)} %param.6) | copy-start | bytes 3076
  7.2 40.2 %all-gather.3.cloned.1.call-start = ((), (), s32[]{:S(2)}) async-start(), calls=%async_computation.2 | async-start | bytes 5242880 | tf_op jit(solution)/shard_map/all_gather | solution.py:19
  52.2 7.6 %copy-start = (bf16[128,512]{1,0:T(8,128)(2,1)S(1)}, bf16[128,512]{1,0:T(8,128)(2,1)}, u32[]{:S(2)}) copy-start(bf16[128,512]{1,0:T(8,128)(2,1)} %param.7) | copy-start | bytes 393220
  64.8 21.6 %all-to-all-start = ((bf16[128,4,1024]{0,2,1:T(8,128)(2,1)}), bf16[128,4,1024]{0,2,1:T(8,128)(2,1)S(1)}, u32[]{:S(2)}, u32[]{:S(2)}) async-start(bf16[128,4,1024]{0,2,1:T(8,128)(2,1)} %bitcast.3), calls=%async_computation | async-start | bytes 2097152 | tf_op jit(solution)/shard_map/all_to_all | solution.py:29
  68.3 89.9 %reduce-scatter.2.cloned.1.call-start = ((), (), s32[]{:S(2)}) async-start(), calls=%async_computation.3 | async-start | bytes 2359296 | tf_op jit(solution)/shard_map/reduce_scatter | solution.py:39
Sparse Core Ops, SparseCore 0:
  10.1 37.1 all-gather.2
  89.7 68.3 reduce-scatter.1
where the time goes:
time: 165 us
  waiting for transfers between devices  92.8 us (56%)
  blocking collectives  24 us (15%)
  between operations  14.1 us (9%)
  local copies, waits for them, and re-layouts  13 us (8%)
  other arithmetic  8.96 us (5%)
  matrix products  8.6 us (5%)
  starting transfers between devices  3.59 us (2%)
    reduce_scatter x1, waiting for transfers between devices, local(): lax.psum_scatter(group_sum, 'outer', scatter_dimension=0, tiled=True)  63.3 us
    all_gather x1, waiting for transfers between devices, local(): code_piece = lax.all_gather(packed, 'inner', axis=0, tiled=True)  29.4 us
    all_gather x1, blocking collectives, local(): piece = lax.all_gather(cotangent, 'inner', axis=0, tiled=True)  18 us
    convert_element_type x1, local copies, waits for them, and re-layouts, local(): dequant = dequant.astype(jnp.bfloat16)  7.57 us
    all_gather x1, blocking collectives, local(): all_scales = lax.all_gather(scales, 'inner', axis=0, tiled=True)  6.02 us
    convert_element_type x1, other arithmetic, local(): dequant = dequant.astype(jnp.bfloat16)  4.89 us
    dot_general x1, matrix products, local(): key_total = jnp.dot(normed, dequant, preferred_element_type=jnp.float32)  3.91 us
    all_to_all x1, starting transfers between devices, local(): lax.all_to_all(normed, 'inner', split_axis=1, concat_axis=0, tiled=True)  3.51 us
  transfers between devices with their start and end apart: 3, of which 2 were waited for; matrix products, arithmetic and copies ran while one was open for 4% of the time, Pallas kernels for 0%

commit v1 on v0

v1 whole, which is shorter than its diff:
```python
import functools

import jax
import jax.numpy as jnp
from jax import lax
from jax.experimental import pallas as pl
from jax.experimental.pallas import tpu as pltpu
from jax.sharding import PartitionSpec as P

EPS = 1e-05
LANES = 128
F32, BF16 = jnp.float32, jnp.bfloat16
VMEM = pl.BlockSpec(memory_space=pltpu.VMEM)
SMEM = pl.BlockSpec(memory_space=pltpu.SMEM)


def call(body, ins, outs, smem=0, flops=0, limit=24):
    specs = [SMEM] * smem + [VMEM] * (len(ins) - smem)
    moved = sum(a.size * a.dtype.itemsize for a in [*ins, *outs])
    return pl.pallas_call(
        body,
        out_shape=outs,
        in_specs=specs,
        out_specs=[VMEM] * len(outs),
        cost_estimate=pl.CostEstimate(flops=max(flops, 4 * moved), bytes_accessed=moved, transcendentals=0),
        compiler_params=pltpu.CompilerParams(vmem_limit_bytes=limit * 1024 * 1024),
    )(*ins)


def dot(a, b, ca, cb):
    return lax.dot_general(a, b, (((ca,), (cb,)), ((), ())), preferred_element_type=F32)


def norm_body(n, m, width, pos, x_ref, inv_ref, *outs):
    x = x_ref[...].astype(F32)
    inv = lax.rsqrt(jnp.mean(x * x, axis=-1, keepdims=True) + EPS)
    inv_ref[...] = jnp.broadcast_to(inv, inv_ref.shape)
    for r in range(n):
        for c in range(2):
            for z in range(m // 2):
                block = (pos[0] ^ r) * m + 2 * z + (pos[1] ^ (1 - c))
                src = pl.multiple_of(block * width, LANES)
                piece = x_ref[:, pl.ds(src, width)].astype(F32) * inv
                outs[2 * r + c][:, z * width : (z + 1) * width] = piece.astype(BF16)


def weight_body(m, width, pos, codes_ref, scales_ref, out_ref):
    rows, groups = codes_ref.shape[0], scales_ref.shape[1]
    per = rows // groups
    for c in range(2):
        for z in range(m // 2):
            block = 2 * z + (pos[1] ^ (1 - c))
            src = pl.multiple_of(block * width, width)
            row = (lax.broadcasted_iota(jnp.int32, (width, groups), 0) + src) // per
            hit = row == lax.broadcasted_iota(jnp.int32, (width, groups), 1)
            scale = jnp.sum(jnp.where(hit, scales_ref[...], 0.0), axis=1, keepdims=True)
            to = (c * (m // 2) + z) * width
            out_ref[to : to + width, :] = (codes_ref[pl.ds(src, width), :].astype(F32) * scale).astype(BF16)


def grad_body(n, w_ref, *refs):
    for ct, out in zip(refs[:n], refs[n:]):
        out[...] = dot(ct[...], w_ref[...], 1, 1).astype(BF16)


def part_body(n, *refs):
    normed, cts, out = refs[:n], refs[n : 2 * n], refs[2 * n]
    total = dot(normed[0][...], cts[0][...], 0, 0)
    for a, b in zip(normed[1:], cts[1:]):
        total += dot(a[...], b[...], 0, 0)
    out[...] = total.astype(out.dtype)


def keys_body(n, w_ref, *refs):
    half = w_ref.shape[0] // 2
    for r in range(n):
        a = dot(refs[2 * r][...], w_ref[:half, :], 1, 0) + dot(refs[2 * r + 1][...], w_ref[half:, :], 1, 0)
        refs[2 * n + r][...] = a.astype(refs[2 * n + r].dtype)


def fold_body(width, k, pos, mine_ref, got_ref, own_ref, *outs):
    for r in range(k):
        at = pl.ds(pl.multiple_of((pos[2] ^ r) * width, width), width)
        total = mine_ref[at, :] + got_ref[at, :].astype(F32)
        if r == 0:
            own_ref[...] = total
        else:
            outs[r - 1][...] = total.astype(BF16)


def sum_body(*refs):
    total = refs[0][...].astype(F32)
    for a in refs[1:-1]:
        total += a[...].astype(F32)
    refs[-1][...] = total.astype(refs[-1].dtype)


def finish_body(n, m, width, pos, x_ref, inv_ref, *refs):
    gns, out = refs[:n], refs[n]
    inv = inv_ref[:, :1]
    total = jnp.zeros((x_ref.shape[0], width), F32)

    def place(r, c, z):
        block = (pos[0] ^ r) * m + 2 * z + (pos[1] ^ (1 - c))
        src = pl.ds(pl.multiple_of(block * width, LANES), width)
        at = (c * (m // 2) + z) * width
        return src, gns[r][:, at : at + width].astype(F32)

    every = [(r, c, z) for r in range(n) for c in range(2) for z in range(m // 2)]
    for r, c, z in every:
        src, gn = place(r, c, z)
        total += gn * (x_ref[:, src].astype(F32) * inv)
    mean = jnp.sum(total, axis=-1, keepdims=True) / x_ref.shape[1]
    for r, c, z in every:
        src, gn = place(r, c, z)
        out[:, src] = (inv * (gn - x_ref[:, src].astype(F32) * inv * mean)).astype(BF16)


def direct(n, m, tokens, codes, scales, ct):
    toks, feats = tokens.shape
    kv = ct.shape[1]
    rows = codes.shape[0]
    width, k = rows // m, m // 2
    i, o = lax.axis_index("inner"), lax.axis_index("outer")
    pos = jnp.stack([i, o % 2, o // 2]).astype(jnp.int32)
    sds = jax.ShapeDtypeStruct

    def inner(a, r):
        return lax.ppermute(a, "inner", [(s, s ^ r) for s in range(n)])

    def outer(a, r):
        return lax.ppermute(a, "outer", [(s, s ^ r) for s in range(m)])

    cts = [ct] + [None] * (n - 1)
    for r in range(2, n, 2):
        cts[r] = inner(ct, r)
    inv, *normed = call(
        functools.partial(norm_body, n, m, width),
        [pos, tokens],
        [sds((toks, LANES), F32)] + [sds((toks, k * width), BF16)] * (2 * n),
        smem=1,
    )
    for r in range(0, n, 2):
        cts[r + 1] = inner(cts[r], 1)
    got = [[normed[c]] + [inner(normed[2 * r + c], r) for r in range(1, n)] for c in range(2)]
    (weight,) = call(
        functools.partial(weight_body, m, width), [pos, codes, scales[None, :]], [sds((rows, kv), BF16)], smem=1
    )
    gns = call(
        functools.partial(grad_body, n),
        [weight, *cts],
        [sds((toks, rows), BF16)] * n,
        flops=2 * n * toks * kv * rows,
    )
    flops = 2 * n * toks * kv * rows // 2
    (far,) = call(functools.partial(part_body, n), [*got[0], *cts], [sds((rows // 2, kv), BF16)], flops=flops)
    far = outer(far, 1)
    (near,) = call(functools.partial(part_body, n), [*got[1], *cts], [sds((rows // 2, kv), F32)], flops=flops)
    both = [got[c][r] for r in range(n) for c in range(2)]
    keys = call(
        functools.partial(keys_body, n),
        [weight, *both],
        [sds((toks, kv), F32)] + [sds((toks, kv), BF16)] * (n - 1),
        flops=2 * flops,
    )
    own, *rest = call(
        functools.partial(fold_body, width, k),
        [pos, near, far],
        [sds((width, kv), F32)] + [sds((width, kv), BF16)] * (k - 1),
        smem=1,
    )
    rest = [outer(a, 2 * r) for r, a in enumerate(rest, 1)]
    gns = [gns[0]] + [inner(gns[r], r) for r in range(1, n)]
    keys = [keys[0]] + [inner(keys[r], r) for r in range(1, n)]
    (grad_weight,) = call(sum_body, [own, *rest], [sds((width, kv), F32)])
    (keys,) = call(sum_body, keys, [sds((toks, kv), BF16)])
    (grad_tokens,) = call(
        functools.partial(finish_body, n, m, width), [pos, tokens, inv, *gns], [sds((toks, feats), BF16)], smem=1
    )
    return keys, grad_tokens, grad_weight


def gathered(tokens, weight_codes, scales, cotangent):
    kv_width = cotangent.shape[1]
    tok_rows = tokens.shape[0]
    xf = tokens.astype(F32)
    inv_norm = lax.rsqrt(jnp.mean(xf * xf, axis=-1, keepdims=True) + EPS)
    normed_f = xf * inv_norm
    normed = normed_f.astype(BF16)
    scale = jnp.repeat(scales, weight_codes.shape[0] // scales.shape[0])
    piece = (weight_codes.astype(F32) * scale[:, None]).astype(BF16)
    weight = lax.all_gather(piece, "inner", axis=0, tiled=True)
    keys = jnp.dot(normed, weight, preferred_element_type=F32).astype(BF16)
    grad_normed = dot(cotangent, weight, 1, 1)
    slab = lax.all_to_all(normed, "inner", split_axis=1, concat_axis=0, tiled=True)
    grads = lax.all_gather(cotangent, "inner", axis=0, tiled=True)
    grad_weight = lax.psum_scatter(dot(slab, grads, 0, 0), "outer", scatter_dimension=0, tiled=True)
    inner_mean = jnp.mean(grad_normed * normed_f, axis=-1, keepdims=True)
    grad_tokens = (inv_norm * (grad_normed - normed_f * inner_mean)).astype(BF16)
    return keys, grad_tokens, grad_weight


def solution(mesh):
    n, m = mesh.shape["inner"], mesh.shape["outer"]

    def local(tokens, weight_codes, scales, cotangent):
        width = weight_codes.shape[0] // m
        powers = n & (n - 1) == 0 and m & (m - 1) == 0
        if powers and 2 <= n <= 8 and 2 <= m <= 16 and width % LANES == 0:
            return direct(n, m, tokens, weight_codes, scales, cotangent)
        return gathered(tokens, weight_codes, scales, cotangent)

    in_specs = (
        P(("inner", "outer"), None),
        P("inner", None),
        P("inner"),
        P(("inner", "outer"), None),
    )
    out_specs = (P(("inner", "outer"), None),) * 3
    return jax.shard_map(local, mesh=mesh, in_specs=in_specs, out_specs=out_specs, check_vma=False)
```

time: 165 us -> 61.7 us (0.37)
  waiting for transfers between devices: 92.8 us -> 28.4 us
  blocking collectives: 24 us -> 0 us
  starting transfers between devices: 3.59 us -> 19.4 us
  between operations: 14.1 us -> 0.74 us
  local copies, waits for them, and re-layouts: 13 us -> 1.25 us
  Pallas kernels: 0 us -> 10.7 us
  other arithmetic: 8.96 us -> 0.08 us
  matrix products: 8.6 us -> 0 us
    reduce_scatter x1 -> x0, waiting for transfers between devices: 63.3 us -> none  [local(): lax.psum_scatter(group_sum, 'outer', scatter_dimension=0, tiled=True)]
    all_gather x1 -> x0, waiting for transfers between devices: 29.4 us -> none  [local(): code_piece = lax.all_gather(packed, 'inner', axis=0, tiled=True)]
    ppermute x0 -> x19, waiting for transfers between devices: none -> 28.4 us  [the longest x15 23 us: inner(): return lax.ppermute(a, 'inner', [(s, s ^ r) for s in range(n)])]
    all_gather x2 -> x0, blocking collectives: 24 us -> none  [the longest x1 18 us: local(): piece = lax.all_gather(cotangent, 'inner', axis=0, tiled=True)]
    ppermute x0 -> x19, starting transfers between devices: none -> 19.4 us  [the longest x15 12.3 us: inner(): return lax.ppermute(a, 'inner', [(s, s ^ r) for s in range(n)])]
    pallas_call x0 -> x10, Pallas kernels: none -> 10.7 us  [call(): pl.pallas_call(body, out_shape=outs, in_specs=specs, out_specs=[VMEM] * l...]
    dot_general x3 -> x0, matrix products: 8.6 us -> none  [the longest x1 3.91 us: local(): key_total = jnp.dot(normed, dequant, preferred_element_type=jnp.float32)]
    convert_element_type x1 -> x0, local copies, waits for them, and re-layouts: 7.57 us -> none  [local(): dequant = dequant.astype(jnp.bfloat16)]
  transfers between devices with their start and end apart: 3 -> 19, of which waited for: 2 -> 7; matrix products, arithmetic and copies ran while one was open for 4% -> 0% of each run, Pallas kernels for 0% -> 15%
where the time goes in v1:
time: 61.7 us; the launch traced here: 60.6 us
  waiting for transfers between devices  28.4 us (46%)
  starting transfers between devices  19.4 us (31%)
  Pallas kernels  10.7 us (17%)
  local copies, waits for them, and re-layouts  1.25 us (2%)
  between operations  0.74 us (1%)
    ppermute x15, waiting for transfers between devices, inner(): return lax.ppermute(a, 'inner', [(s, s ^ r) for s in range(n)])  23 us
    ppermute x15, starting transfers between devices, inner(): return lax.ppermute(a, 'inner', [(s, s ^ r) for s in range(n)])  12.3 us
    pallas_call x10, Pallas kernels, call(): pl.pallas_call(body, out_shape=outs, in_specs=specs, out_specs=[VMEM] * l...  10.7 us
    ppermute x4, starting transfers between devices, outer(): return lax.ppermute(a, 'outer', [(s, s ^ r) for s in range(m)])  7.09 us
    ppermute x4, waiting for transfers between devices, outer(): return lax.ppermute(a, 'outer', [(s, s ^ r) for s in range(m)])  5.47 us
    unnamed x10, local copies, waits for them, and re-layouts  1.25 us
  transfers between devices with their start and end apart: 19, of which 7 were waited for; matrix products, arithmetic and copies ran while one was open for 0% of the time, Pallas kernels for 15%

profile of v1, /device:TPU:0, one launch (start us, length us, event | category | flops | bytes accessed | tf_op | source)
XLA Modules:
  0.0 60.6 jit_solution(18418993409382821398)
XLA Ops:
  0.6 3.0 %collective-permute-start.10 = (bf16[128,512]{1,0:T(8,128)(2,1)}, bf16[128,512]{1,0:T(8,128)(2,1)S(1)}, u32[]{:S(2)}, u32[]{:S(2)}) collective-permute-start(bf16[128,512]{1,0:T(8,128)(2,1)} %refs_4_.3), channel_id=1, source_target_pairs={{0,16},{8,24},{16,0},{24,8},{1,17},{9,25},{17,1},{25,9},{2,18},{10... | collective-permute-start | bytes 393224 | tf_op jit(solution)/shard_map/ppermute | solution.py:129
  3.7 0.0 collective-permute-start.9
  3.7 0.1 pad_add_fusion.pos
  3.7 0.0 copy-start
  3.7 1.2 %copy-done = bf16[128,4096]{1,0:T(8,128)(2,1)S(1)} copy-done((bf16[128,4096]{1,0:T(8,128)(2,1)S(1)}, bf16[128,4096]{1,0:T(8,128)(2,1)}, u32[]{:S(2)}) %copy-start) | copy-done | bytes 1048600
  5.0 0.0 copy-start.3
  5.0 1.0 %shard_map.68 = (f32[128,128]{1,0:T(8,128)S(1)}, bf16[128,512]{1,0:T(8,128)(2,1)S(1)}, bf16[128,512]{1,0:T(8,128)(2,1)S(1)}, bf16[128,512]{1,0:T(8,128)(2,1)S(1)...) custom-call(s32[3]{0:T(128)S(1)} %pad_add_fusion.pos, ...), custom_call_target="tpu_custom_call" | custom-call | flops 8650800 | bytes 2162700 | tf_op jit(solution)/shard_map/pallas_call | solution.py:20
  6.0 0.0 copy-start.2
  6.0 0.6 collective-permute-start
  6.6 0.1 collective-permute-start.2
  6.7 1.3 %collective-permute-start.4 = (bf16[128,512]{1,0:T(8,128)(2,1)S(1)}, bf16[128,512]{1,0:T(8,128)(2,1)S(1)}, u32[]{:S(2)}, u32[]{:S(2)}) collective-permute-start(bf16[128,512]{1,0:T(8,128)(2,1)S(1)} %get-tuple-element.30), channel_id=1, source_target_pairs={{0,24},{8,16},{16,8},{24,0},{1,25},{9,17},{17,9},{25,1},{2,26},{10... | collective-permute-start | bytes 393224 | tf_op jit(solution)/shard_map/ppermute | solution.py:129
  8.0 0.0 collective-permute-done.10.refs_2_.refs_6_
  8.0 0.7 %collective-permute-start.11 = (bf16[128,512]{1,0:T(8,128)(2,1)S(1)}, bf16[128,512]{1,0:T(8,128)(2,1)S(1)}, u32[]{:S(2)}, u32[]{:S(2)}) collective-permute-start(bf16[128,512]{1,0:T(8,128)(2,1)S(1)} %collective-permute-done.10.refs_2_.refs_6_), channel_id=1, source_target_pairs={{0,8},{8,0},{16,24},{24,16},{1,9},{9,1},{17,25},{25,17},{2,10},{10... | collective-permute-start | bytes 393224 | tf_op jit(solution)/shard_map/ppermute | solution.py:129
  8.7 0.0 collective-permute-done.refs_2_.refs_1_
  8.7 4.2 %collective-permute-done.2.refs_4_.refs_2_ = bf16[128,512]{1,0:T(8,128)(2,1)S(1)} collective-permute-done((bf16[128,512]{1,0:T(8,128)(2,1)S(1)}, bf16[128,512]{1,0:T(8,128)(2,1)S(1)}, u32[]{:S(2)}, u32[]{:S(2)}) %collective-permute-start.2) | collective-permute-done | bytes 131104 | tf_op jit(solution)/shard_map/ppermute | solution.py:129
  13.0 1.0 %collective-permute-done.4.refs_6_.refs_3_ = bf16[128,512]{1,0:T(8,128)(2,1)S(1)} collective-permute-done((bf16[128,512]{1,0:T(8,128)(2,1)S(1)}, bf16[128,512]{1,0:T(8,128)(2,1)S(1)}, u32[]{:S(2)}, u32[]{:S(2)}) %collective-permute-start.4) | collective-permute-done | bytes 131104 | tf_op jit(solution)/shard_map/ppermute | solution.py:129
  14.0 0.0 collective-permute-done.9.refs_1_.refs_5_
  14.0 0.0 collective-permute-done.11.refs_3_.refs_7_
  14.0 0.0 copy-done.3
  14.0 0.7 %shard_map.74 = bf16[512,512]{1,0:T(8,128)(2,1)S(1)} custom-call(bf16[128,512]{1,0:T(8,128)(2,1)S(1)} %get-tuple-element.24.refs_0_, bf16[128,512]{1,0:T(8,128)(2,1)S(1)} %collective-permute-done.refs_2_.refs_1_, bf16[128,512]{1,0:T(8,128)(2,1)S(1)} %collective-permute-done.2.refs_4_.refs_2_, bf16[128,512]{1,0:T(8,128)(2,1)S(1)} %collective-permute-done.4.refs_6_.refs_3_, ...), custom_call_target="tpu_custom_call" | custom-call | flops 268435456 | bytes 1572864 | tf_op jit(solution)/shard_map/pallas_call | solution.py:20
  14.7 1.6 %collective-permute-start.15 = (bf16[512,512]{1,0:T(8,128)(2,1)S(1)}, bf16[512,512]{1,0:T(8,128)(2,1)S(1)}, u32[]{:S(2)}, u32[]{:S(2)}) collective-permute-start(bf16[512,512]{1,0:T(8,128)(2,1)S(1)} %shard_map.74), channel_id=1, source_target_pairs={{0,1},{1,0},{2,3},{3,2},{4,5},{5,4},{6,7},{7,6},{8,9},{9,8},{10,11... | collective-permute-start | bytes 1572872 | tf_op jit(solution)/shard_map/ppermute | solution.py:132
  16.3 0.4 collective-permute-start.1
  16.8 0.5 collective-permute-start.3
  17.3 0.0 copy-start.4
  17.3 0.9 %collective-permute-start.5 = (bf16[128,512]{1,0:T(8,128)(2,1)S(1)}, bf16[128,512]{1,0:T(8,128)(2,1)S(1)}, u32[]{:S(2)}, u32[]{:S(2)}) collective-permute-start(bf16[128,512]{1,0:T(8,128)(2,1)S(1)} %get-tuple-element.31), channel_id=1, source_target_pairs={{0,24},{8,16},{16,8},{24,0},{1,25},{9,17},{17,9},{25,1},{2,26},{10... | collective-permute-start | bytes 393224 | tf_op jit(solution)/shard_map/ppermute | solution.py:129
  18.2 0.0 copy-done.2
  18.2 0.0 copy-done.4
  18.2 1.1 %shard_map.67.w_ref = bf16[1024,512]{1,0:T(8,128)(2,1)S(1)} custom-call(s32[3]{0:T(128)S(1)} %pad_add_fusion.pos, bf16[1024,512]{1,0:T(8,128)(2,1)S(1)} %copy-done.2, f32[1,256]{1,0:T(1,128)S(1)} %bitcast.4), custom_call_target="tpu_custom_call" | custom-call | flops 8392752 | bytes 2098188 | tf_op jit(solution)/shard_map/pallas_call | solution.py:20
  19.3 0.0 collective-permute-done.1.refs_3_.refs_1_
  19.3 3.8 %collective-permute-done.3.refs_5_.refs_2_ = bf16[128,512]{1,0:T(8,128)(2,1)S(1)} collective-permute-done((bf16[128,512]{1,0:T(8,128)(2,1)S(1)}, bf16[128,512]{1,0:T(8,128)(2,1)S(1)}, u32[]{:S(2)}, u32[]{:S(2)}) %collective-permute-start.3) | collective-permute-done | bytes 131104 | tf_op jit(solution)/shard_map/ppermute | solution.py:129
  23.1 1.0 %collective-permute-done.5.refs_7_.refs_3_ = bf16[128,512]{1,0:T(8,128)(2,1)S(1)} collective-permute-done((bf16[128,512]{1,0:T(8,128)(2,1)S(1)}, bf16[128,512]{1,0:T(8,128)(2,1)S(1)}, u32[]{:S(2)}, u32[]{:S(2)}) %collective-permute-start.5) | collective-permute-done | bytes 131104 | tf_op jit(solution)/shard_map/ppermute | solution.py:129
  24.1 0.7 %shard_map.69 = (f32[128,512]{1,0:T(8,128)S(1)}, bf16[128,512]{1,0:T(8,128)(2,1)S(1)}, bf16[128,512]{1,0:T(8,128)(2,1)S(1)}, bf16[128,512]{1,0:T(8,128)(2,1)S(1)}) custom-call(bf16[1024,512]{1,0:T(8,128)(2,1)S(1)} %shard_map.67.w_ref, bf16[128,512]{1,0:T(8,128)(2,1)S(1)} %get-tuple-element.24.refs_0_, ...), custom_call_target="tpu_custom_call" | custom-call | flops 536870912 | bytes 2752512 | tf_op jit(solution)/shard_map/pallas_call | solution.py:20
  24.9 1.1 %collective-permute-start.6 = (bf16[128,512]{1,0:T(8,128)(2,1)S(1)}, bf16[128,512]{1,0:T(8,128)(2,1)S(1)}, u32[]{:S(2)}, u32[]{:S(2)}) collective-permute-start(bf16[128,512]{1,0:T(8,128)(2,1)S(1)} %get-tuple-element.33), channel_id=1, source_target_pairs={{0,8},{8,0},{16,24},{24,16},{1,9},{9,1},{17,25},{25,17},{2,10},{10... | collective-permute-start | bytes 393224 | tf_op jit(solution)/shard_map/ppermute | solution.py:129
  25.9 1.5 %shard_map.71 = (bf16[128,1024]{1,0:T(8,128)(2,1)S(1)}, bf16[128,1024]{1,0:T(8,128)(2,1)S(1)}, bf16[128,1024]{1,0:T(8,128)(2,1)S(1)}, bf16[128,1024]{1,0:T(8,128)(2,1)S(1)}) custom-call(bf16[1024,512]{1,0:T(8,128)(2,1)S(1)} %shard_map.67.w_ref, bf16[128,512]{1,0:T(8,128)(2,1)S(1)} %copy-done.3, bf16[128,512]{1,0:T(8,128)(2,1)S(1)} %collective-permute-done.9.refs_1_.refs_5_, ...), custom_call_target="tpu_custom_call" | custom-call | flops 536870912 | bytes 2621440 | tf_op jit(solution)/shard_map/pallas_call | solution.py:20
  27.4 0.1 collective-permute-start.12
  27.5 0.6 collective-permute-start.13
  28.1 1.3 %collective-permute-start.14 = (bf16[128,1024]{1,0:T(8,128)(2,1)S(1)}, bf16[128,1024]{1,0:T(8,128)(2,1)S(1)}, u32[]{:S(2)}, u32[]{:S(2)}) collective-permute-start(bf16[128,1024]{1,0:T(8,128)(2,1)S(1)} %get-tuple-element.40), channel_id=1, source_target_pairs={{0,24},{8,16},{16,8},{24,0},{1,25},{9,17},{17,9},{25,1},{2,26},{10... | collective-permute-start | bytes 786440 | tf_op jit(solution)/shard_map/ppermute | solution.py:129
  29.4 0.0 collective-permute-done.6.refs_1_
  29.4 0.5 collective-permute-start.7
  29.9 0.0 collective-permute-done.15.got_ref
  29.9 1.2 %collective-permute-start.8 = (bf16[128,512]{1,0:T(8,128)(2,1)S(1)}, bf16[128,512]{1,0:T(8,128)(2,1)S(1)}, u32[]{:S(2)}, u32[]{:S(2)}) collective-permute-start(bf16[128,512]{1,0:T(8,128)(2,1)S(1)} %get-tuple-element.35), channel_id=1, source_target_pairs={{0,24},{8,16},{16,8},{24,0},{1,25},{9,17},{17,9},{25,1},{2,26},{10... | collective-permute-start | bytes 393224 | tf_op jit(solution)/shard_map/ppermute | solution.py:129
  31.1 0.7 %shard_map.73.mine_ref = f32[512,512]{1,0:T(8,128)S(1)} custom-call(bf16[128,512]{1,0:T(8,128)(2,1)S(1)} %get-tuple-element.25.refs_1_.refs_0_, bf16[128,512]{1,0:T(8,128)(2,1)S(1)} %collective-permute-done.1.refs_3_.refs_1_, bf16[128,512]{1,0:T(8,128)(2,1)S(1)} %collective-permute-done.3.refs_5_.refs_2_, ...), custom_call_target="tpu_custom_call" | custom-call | flops 268435456 | bytes 2097152 | tf_op jit(solution)/shard_map/pallas_call | solution.py:20
  31.8 0.0 copy-start.1
  31.8 0.6 %shard_map.75 = (f32[128,512]{1,0:T(8,128)S(1)}, bf16[128,512]{1,0:T(8,128)(2,1)S(1)}, bf16[128,512]{1,0:T(8,128)(2,1)S(1)}, bf16[128,512]{1,0:T(8,128)(2,1)S(1)}) custom-call(s32[3]{0:T(128)S(1)} %pad_add_fusion.pos, f32[512,512]{1,0:T(8,128)S(1)} %shard_map.73.mine_ref, bf16[512,512]{1,0:T(8,128)(2,1)S(1)} %collective-permute-done.15.got_ref), custom_call_target="tpu_custom_call" | custom-call | flops 8912944 | bytes 2228236 | tf_op jit(solution)/shard_map/pallas_call | solution.py:20
  32.5 12.7 %collective-permute-done.7.refs_2_ = bf16[128,512]{1,0:T(8,128)(2,1)S(1)} collective-permute-done((bf16[128,512]{1,0:T(8,128)(2,1)S(1)}, bf16[128,512]{1,0:T(8,128)(2,1)S(1)}, u32[]{:S(2)}, u32[]{:S(2)}) %collective-permute-start.7) | collective-permute-done | bytes 131104 | tf_op jit(solution)/shard_map/ppermute | solution.py:129
  45.2 1.6 %collective-permute-start.16 = (bf16[128,512]{1,0:T(8,128)(2,1)S(1)}, bf16[128,512]{1,0:T(8,128)(2,1)S(1)}, u32[]{:S(2)}, u32[]{:S(2)}) collective-permute-start(bf16[128,512]{1,0:T(8,128)(2,1)S(1)} %get-tuple-element.42), channel_id=1, source_target_pairs={{0,2},{1,3},{2,0},{3,1},{4,6},{5,7},{6,4},{7,5},{8,10},{9,11},{10,... | collective-permute-start | bytes 393224 | tf_op jit(solution)/shard_map/ppermute | solution.py:132
  46.8 0.2 collective-permute-done.8.refs_3_
  46.9 2.6 %collective-permute-start.17 = (bf16[128,512]{1,0:T(8,128)(2,1)S(1)}, bf16[128,512]{1,0:T(8,128)(2,1)S(1)}, u32[]{:S(2)}, u32[]{:S(2)}) collective-permute-start(bf16[128,512]{1,0:T(8,128)(2,1)S(1)} %get-tuple-element.43), channel_id=1, source_target_pairs={{0,4},{1,5},{2,6},{3,7},{4,0},{5,1},{6,2},{7,3},{8,12},{9,13},{10,... | collective-permute-start | bytes 393224 | tf_op jit(solution)/shard_map/ppermute | solution.py:132
  49.5 0.0 collective-permute-done.12.refs_1_
  49.5 1.3 %collective-permute-start.18 = (bf16[128,512]{1,0:T(8,128)(2,1)S(1)}, bf16[128,512]{1,0:T(8,128)(2,1)S(1)}, u32[]{:S(2)}, u32[]{:S(2)}) collective-permute-start(bf16[128,512]{1,0:T(8,128)(2,1)S(1)} %get-tuple-element.44), channel_id=1, source_target_pairs={{0,6},{1,7},{2,4},{3,5},{4,2},{5,3},{6,0},{7,1},{8,14},{9,15},{10,... | collective-permute-start | bytes 393224 | tf_op jit(solution)/shard_map/ppermute | solution.py:132
  50.9 0.7 %shard_map.70 = bf16[128,512]{1,0:T(8,128)(2,1)} custom-call(f32[128,512]{1,0:T(8,128)S(1)} %get-tuple-element.32.refs_0_, bf16[128,512]{1,0:T(8,128)(2,1)S(1)} %collective-permute-done.6.refs_1_, bf16[128,512]{1,0:T(8,128)(2,1)S(1)} %collective-permute-done.7.refs_2_, bf16[128,512]{1,0:T(8,128)(2,1)S(1)} %collective-permute-done.8.refs_3_), custom_call_target="tpu_custom_call" | custom-call | flops 3145728 | bytes 786432 | tf_op jit(solution)/shard_map/pallas_call | solution.py:20
  51.6 0.0 collective-permute-done.13.refs_2_
  51.6 0.0 collective-permute-done.14.refs_3_
  51.6 0.0 copy-done.1
  51.6 2.7 %shard_map.72 = bf16[128,4096]{1,0:T(8,128)(2,1)} custom-call(s32[3]{0:T(128)S(1)} %pad_add_fusion.pos, bf16[128,4096]{1,0:T(8,128)(2,1)S(1)} %copy-done.1, f32[128,128]{1,0:T(8,128)S(1)} %get-tuple-element.36.inv_ref, bf16[128,1024]{1,0:T(8,128)(2,1)S(1)} %get-tuple-element.37.refs_0_, bf16[128,1024]{1,0:T(8,128)(2,1)S(1)} %collective-permute-done.12.refs_1_, ...), custom_call_target="tpu_custom_call" | custom-call | flops 12845104 | bytes 3211276 | tf_op jit(solution)/shard_map/pallas_call | solution.py:20
  54.3 0.0 collective-permute-done.16.refs_1_
  54.3 5.5 %collective-permute-done.17.refs_2_ = bf16[128,512]{1,0:T(8,128)(2,1)S(1)} collective-permute-done((bf16[128,512]{1,0:T(8,128)(2,1)S(1)}, bf16[128,512]{1,0:T(8,128)(2,1)S(1)}, u32[]{:S(2)}, u32[]{:S(2)}) %collective-permute-start.17) | collective-permute-done | bytes 131104 | tf_op jit(solution)/shard_map/ppermute | solution.py:132
  59.8 0.0 collective-permute-done.18.refs_3_
  59.8 0.8 %shard_map.76 = f32[128,512]{1,0:T(8,128)} custom-call(f32[128,512]{1,0:T(8,128)S(1)} %get-tuple-element.41.refs_0_, bf16[128,512]{1,0:T(8,128)(2,1)S(1)} %collective-permute-done.16.refs_1_, bf16[128,512]{1,0:T(8,128)(2,1)S(1)} %collective-permute-done.17.refs_2_, bf16[128,512]{1,0:T(8,128)(2,1)S(1)} %collective-permute-done.18.refs_3_), custom_call_target="tpu_custom_call" | custom-call | flops 3670016 | bytes 917504 | tf_op jit(solution)/shard_map/pallas_call | solution.py:20
Async XLA Ops:
  0.6 7.4 %collective-permute-start.10 = (bf16[128,512]{1,0:T(8,128)(2,1)}, bf16[128,512]{1,0:T(8,128)(2,1)S(1)}, u32[]{:S(2)}, u32[]{:S(2)}) collective-permute-start(bf16[128,512]{1,0:T(8,128)(2,1)} %refs_4_.3), channel_id=1, source_target_pairs={{0,16},{8,24},{16,0},{24,8},{1,17},{9,25},{17,1},{25,9},{2,18},{10... | collective-permute-start | bytes 393224 | tf_op jit(solution)/shard_map/ppermute | solution.py:129
  3.7 10.3 %collective-permute-start.9 = (bf16[128,512]{1,0:T(8,128)(2,1)}, bf16[128,512]{1,0:T(8,128)(2,1)S(1)}, u32[]{:S(2)}, u32[]{:S(2)}) collective-permute-start(bf16[128,512]{1,0:T(8,128)(2,1)} %refs_4_.3), channel_id=1, source_target_pairs={{0,8},{8,0},{16,24},{24,16},{1,9},{9,1},{17,25},{25,17},{2,10},{10... | collective-permute-start | bytes 393224 | tf_op jit(solution)/shard_map/ppermute | solution.py:129
  3.7 1.2 %copy-start = (bf16[128,4096]{1,0:T(8,128)(2,1)S(1)}, bf16[128,4096]{1,0:T(8,128)(2,1)}, u32[]{:S(2)}) copy-start(bf16[128,4096]{1,0:T(8,128)(2,1)} %x_ref.3) | copy-start | bytes 3145732
  5.0 9.0 %copy-start.3 = (bf16[128,512]{1,0:T(8,128)(2,1)S(1)}, bf16[128,512]{1,0:T(8,128)(2,1)}, u32[]{:S(2)}) copy-start(bf16[128,512]{1,0:T(8,128)(2,1)} %refs_4_.3) | copy-start | bytes 393220
  6.0 12.2 %copy-start.2 = (bf16[1024,512]{1,0:T(8,128)(2,1)S(1)}, bf16[1024,512]{1,0:T(8,128)(2,1)}, u32[]{:S(2)}) copy-start(bf16[1024,512]{1,0:T(8,128)(2,1)} %codes_ref.1) | copy-start | bytes 3145732
  6.0 2.7 %collective-permute-start = (bf16[128,512]{1,0:T(8,128)(2,1)S(1)}, bf16[128,512]{1,0:T(8,128)(2,1)S(1)}, u32[]{:S(2)}, u32[]{:S(2)}) collective-permute-start(bf16[128,512]{1,0:T(8,128)(2,1)S(1)} %get-tuple-element.26), channel_id=1, source_target_pairs={{0,8},{8,0},{16,24},{24,16},{1,9},{9,1},{17,25},{25,17},{2,10},{10... | collective-permute-start | bytes 393224 | tf_op jit(solution)/shard_map/ppermute | solution.py:129
  6.6 6.4 %collective-permute-start.2 = (bf16[128,512]{1,0:T(8,128)(2,1)S(1)}, bf16[128,512]{1,0:T(8,128)(2,1)S(1)}, u32[]{:S(2)}, u32[]{:S(2)}) collective-permute-start(bf16[128,512]{1,0:T(8,128)(2,1)S(1)} %get-tuple-element.28), channel_id=1, source_target_pairs={{0,16},{8,24},{16,0},{24,8},{1,17},{9,25},{17,1},{25,9},{2,18},{10... | collective-permute-start | bytes 393224 | tf_op jit(solution)/shard_map/ppermute | solution.py:129
  6.7 7.3 %collective-permute-start.4 = (bf16[128,512]{1,0:T(8,128)(2,1)S(1)}, bf16[128,512]{1,0:T(8,128)(2,1)S(1)}, u32[]{:S(2)}, u32[]{:S(2)}) collective-permute-start(bf16[128,512]{1,0:T(8,128)(2,1)S(1)} %get-tuple-element.30), channel_id=1, source_target_pairs={{0,24},{8,16},{16,8},{24,0},{1,25},{9,17},{17,9},{25,1},{2,26},{10... | collective-permute-start | bytes 393224 | tf_op jit(solution)/shard_map/ppermute | solution.py:129
  8.0 6.0 %collective-permute-start.11 = (bf16[128,512]{1,0:T(8,128)(2,1)S(1)}, bf16[128,512]{1,0:T(8,128)(2,1)S(1)}, u32[]{:S(2)}, u32[]{:S(2)}) collective-permute-start(bf16[128,512]{1,0:T(8,128)(2,1)S(1)} %collective-permute-done.10.refs_2_.refs_6_), channel_id=1, source_target_pairs={{0,8},{8,0},{16,24},{24,16},{1,9},{9,1},{17,25},{25,17},{2,10},{10... | collective-permute-start | bytes 393224 | tf_op jit(solution)/shard_map/ppermute | solution.py:129
  14.7 15.2 %collective-permute-start.15 = (bf16[512,512]{1,0:T(8,128)(2,1)S(1)}, bf16[512,512]{1,0:T(8,128)(2,1)S(1)}, u32[]{:S(2)}, u32[]{:S(2)}) collective-permute-start(bf16[512,512]{1,0:T(8,128)(2,1)S(1)} %shard_map.74), channel_id=1, source_target_pairs={{0,1},{1,0},{2,3},{3,2},{4,5},{5,4},{6,7},{7,6},{8,9},{9,8},{10,11... | collective-permute-start | bytes 1572872 | tf_op jit(solution)/shard_map/ppermute | solution.py:132
  16.3 3.0 %collective-permute-start.1 = (bf16[128,512]{1,0:T(8,128)(2,1)S(1)}, bf16[128,512]{1,0:T(8,128)(2,1)S(1)}, u32[]{:S(2)}, u32[]{:S(2)}) collective-permute-start(bf16[128,512]{1,0:T(8,128)(2,1)S(1)} %get-tuple-element.27), channel_id=1, source_target_pairs={{0,8},{8,0},{16,24},{24,16},{1,9},{9,1},{17,25},{25,17},{2,10},{10... | collective-permute-start | bytes 393224 | tf_op jit(solution)/shard_map/ppermute | solution.py:129
  16.8 6.4 %collective-permute-start.3 = (bf16[128,512]{1,0:T(8,128)(2,1)S(1)}, bf16[128,512]{1,0:T(8,128)(2,1)S(1)}, u32[]{:S(2)}, u32[]{:S(2)}) collective-permute-start(bf16[128,512]{1,0:T(8,128)(2,1)S(1)} %get-tuple-element.29), channel_id=1, source_target_pairs={{0,16},{8,24},{16,0},{24,8},{1,17},{9,25},{17,1},{25,9},{2,18},{10... | collective-permute-start | bytes 393224 | tf_op jit(solution)/shard_map/ppermute | solution.py:129
  17.3 0.9 %copy-start.4 = (f32[256]{0:T(256)S(1)}, f32[256]{0:T(256)}, u32[]{:S(2)}) copy-start(f32[256]{0:T(256)} %param.6) | copy-start | bytes 3076
  17.3 6.8 %collective-permute-start.5 = (bf16[128,512]{1,0:T(8,128)(2,1)S(1)}, bf16[128,512]{1,0:T(8,128)(2,1)S(1)}, u32[]{:S(2)}, u32[]{:S(2)}) collective-permute-start(bf16[128,512]{1,0:T(8,128)(2,1)S(1)} %get-tuple-element.31), channel_id=1, source_target_pairs={{0,24},{8,16},{16,8},{24,0},{1,25},{9,17},{17,9},{25,1},{2,26},{10... | collective-permute-start | bytes 393224 | tf_op jit(solution)/shard_map/ppermute | solution.py:129
  24.9 4.5 %collective-permute-start.6 = (bf16[128,512]{1,0:T(8,128)(2,1)S(1)}, bf16[128,512]{1,0:T(8,128)(2,1)S(1)}, u32[]{:S(2)}, u32[]{:S(2)}) collective-permute-start(bf16[128,512]{1,0:T(8,128)(2,1)S(1)} %get-tuple-element.33), channel_id=1, source_target_pairs={{0,8},{8,0},{16,24},{24,16},{1,9},{9,1},{17,25},{25,17},{2,10},{10... | collective-permute-start | bytes 393224 | tf_op jit(solution)/shard_map/ppermute | solution.py:129
  27.4 22.1 %collective-permute-start.12 = (bf16[128,1024]{1,0:T(8,128)(2,1)S(1)}, bf16[128,1024]{1,0:T(8,128)(2,1)S(1)}, u32[]{:S(2)}, u32[]{:S(2)}) collective-permute-start(bf16[128,1024]{1,0:T(8,128)(2,1)S(1)} %get-tuple-element.38), channel_id=1, source_target_pairs={{0,8},{8,0},{16,24},{24,16},{1,9},{9,1},{17,25},{25,17},{2,10},{10... | collective-permute-start | bytes 786440 | tf_op jit(solution)/shard_map/ppermute | solution.py:129
  27.5 24.1 %collective-permute-start.13 = (bf16[128,1024]{1,0:T(8,128)(2,1)S(1)}, bf16[128,1024]{1,0:T(8,128)(2,1)S(1)}, u32[]{:S(2)}, u32[]{:S(2)}) collective-permute-start(bf16[128,1024]{1,0:T(8,128)(2,1)S(1)} %get-tuple-element.39), channel_id=1, source_target_pairs={{0,16},{8,24},{16,0},{24,8},{1,17},{9,25},{17,1},{25,9},{2,18},{10... | collective-permute-start | bytes 786440 | tf_op jit(solution)/shard_map/ppermute | solution.py:129
  28.1 23.5 %collective-permute-start.14 = (bf16[128,1024]{1,0:T(8,128)(2,1)S(1)}, bf16[128,1024]{1,0:T(8,128)(2,1)S(1)}, u32[]{:S(2)}, u32[]{:S(2)}) collective-permute-start(bf16[128,1024]{1,0:T(8,128)(2,1)S(1)} %get-tuple-element.40), channel_id=1, source_target_pairs={{0,24},{8,16},{16,8},{24,0},{1,25},{9,17},{17,9},{25,1},{2,26},{10... | collective-permute-start | bytes 786440 | tf_op jit(solution)/shard_map/ppermute | solution.py:129
  29.4 15.8 %collective-permute-start.7 = (bf16[128,512]{1,0:T(8,128)(2,1)S(1)}, bf16[128,512]{1,0:T(8,128)(2,1)S(1)}, u32[]{:S(2)}, u32[]{:S(2)}) collective-permute-start(bf16[128,512]{1,0:T(8,128)(2,1)S(1)} %get-tuple-element.34), channel_id=1, source_target_pairs={{0,16},{8,24},{16,0},{24,8},{1,17},{9,25},{17,1},{25,9},{2,18},{10... | collective-permute-start | bytes 393224 | tf_op jit(solution)/shard_map/ppermute | solution.py:129
  29.9 17.0 %collective-permute-start.8 = (bf16[128,512]{1,0:T(8,128)(2,1)S(1)}, bf16[128,512]{1,0:T(8,128)(2,1)S(1)}, u32[]{:S(2)}, u32[]{:S(2)}) collective-permute-start(bf16[128,512]{1,0:T(8,128)(2,1)S(1)} %get-tuple-element.35), channel_id=1, source_target_pairs={{0,24},{8,16},{16,8},{24,0},{1,25},{9,17},{17,9},{25,1},{2,26},{10... | collective-permute-start | bytes 393224 | tf_op jit(solution)/shard_map/ppermute | solution.py:129
  31.8 19.8 %copy-start.1 = (bf16[128,4096]{1,0:T(8,128)(2,1)S(1)}, bf16[128,4096]{1,0:T(8,128)(2,1)}, u32[]{:S(2)}) copy-start(bf16[128,4096]{1,0:T(8,128)(2,1)} %x_ref.3) | copy-start | bytes 3145732
  45.2 9.1 %collective-permute-start.16 = (bf16[128,512]{1,0:T(8,128)(2,1)S(1)}, bf16[128,512]{1,0:T(8,128)(2,1)S(1)}, u32[]{:S(2)}, u32[]{:S(2)}) collective-permute-start(bf16[128,512]{1,0:T(8,128)(2,1)S(1)} %get-tuple-element.42), channel_id=1, source_target_pairs={{0,2},{1,3},{2,0},{3,1},{4,6},{5,7},{6,4},{7,5},{8,10},{9,11},{10,... | collective-permute-start | bytes 393224 | tf_op jit(solution)/shard_map/ppermute | solution.py:132
  46.9 12.9 %collective-permute-start.17 = (bf16[128,512]{1,0:T(8,128)(2,1)S(1)}, bf16[128,512]{1,0:T(8,128)(2,1)S(1)}, u32[]{:S(2)}, u32[]{:S(2)}) collective-permute-start(bf16[128,512]{1,0:T(8,128)(2,1)S(1)} %get-tuple-element.43), channel_id=1, source_target_pairs={{0,4},{1,5},{2,6},{3,7},{4,0},{5,1},{6,2},{7,3},{8,12},{9,13},{10,... | collective-permute-start | bytes 393224 | tf_op jit(solution)/shard_map/ppermute | solution.py:132
  49.5 10.3 %collective-permute-start.18 = (bf16[128,512]{1,0:T(8,128)(2,1)S(1)}, bf16[128,512]{1,0:T(8,128)(2,1)S(1)}, u32[]{:S(2)}, u32[]{:S(2)}) collective-permute-start(bf16[128,512]{1,0:T(8,128)(2,1)S(1)} %get-tuple-element.44), channel_id=1, source_target_pairs={{0,6},{1,7},{2,4},{3,5},{4,2},{5,3},{6,0},{7,1},{8,14},{9,15},{10,... | collective-permute-start | bytes 393224 | tf_op jit(solution)/shard_map/ppermute | solution.py:132
